TPU v7x, 32 devices: a whole 2x2x4 slice. The times are simulated.
32 devices in a mesh: gy: 4 (over z), gx: 8 (over y, x, core).
Axes of the slice: x: 2, y: 2, z: 4, core: 2. Of those that a mesh axis runs over, the one named last changes fastest.
Arguments:
- coefficients: float32 [9, 128, 256], P(None, 'gy', 'gx'), may hold values from -2.1 to 2.1
- vectors: float32 [128, 256, 2048], P('gy', 'gx'), may hold values from -6 to 6
Outputs:
- normal: float32 [25, 128, 256], P(None, 'gy', 'gx')
- image: float32 [128, 256, 2048], P('gy', 'gx')
All inputs are finite; a program needn't handle non-finite values.
Results may differ from a plain program's by a relative error of at most 0.00002.
Values sent between devices are 32-bit elements; how exact they have to be, the bound alone decides.
A program may use at most 192 MiB of HBM per device.

v0:
```python
import functools
import jax
import jax.numpy as jnp
from jax import lax
from jax.experimental import pallas as pl
from jax.experimental.pallas import tpu as pltpu
from jax.sharding import PartitionSpec as P

MESH = pl.DeviceIdType.MESH
GROUP = 4
LANES = 256


DIRECTIONS = ((1, 0), (-1, 0), (0, 1), (0, -1), (1, 1), (1, -1), (-1, 1), (-1, -1))


def exchange_kernel(ny, nx, x_ref, first_ref, last_ref, strips_ref, up, down, left, right, near, zero, *sems):
    send_sem, recv_sem, strip_send, strip_recv, fill_sem = sems
    rows = x_ref.shape[0]
    gy = lax.axis_index("gy")
    gx = lax.axis_index("gx")

    def there(dy, dx):
        y = gy + dy
        x = gx + dx
        return (y >= 0) & (y < ny) & (x >= 0) & (x < nx)

    barrier = pltpu.get_barrier_semaphore()
    count = jnp.int32(0)
    for dy, dx in DIRECTIONS:
        count = count + there(dy, dx).astype(jnp.int32)

        @pl.when(there(dy, dx))
        def _():
            pl.semaphore_signal(barrier, inc=1, device_id={"gy": gy + dy, "gx": gx + dx}, device_id_type=MESH)

    pl.semaphore_wait(barrier, count)

    mine = {1: pl.ds(rows - 2, 2), -1: pl.ds(0, 2)}
    land = {1: pl.ds(0, 2), 0: pl.ds(2, rows), -1: pl.ds(rows + 2, 2)}
    jobs = []
    for d, (dy, dx) in enumerate(DIRECTIONS):
        to = {"gy": gy + dy, "gx": gx + dx}
        if dx == 0:
            source = x_ref.at[mine[dy]]
            target = up if dy > 0 else down
        else:
            column = last_ref if dx > 0 else first_ref
            source = column.at[mine[dy]] if dy else column
            target = (left if dx > 0 else right).at[land[dy]]
        strip = (dy + 1) // 2 if dy else 2 + (dx + 1) // 2
        small = pltpu.make_async_remote_copy(
            strips_ref.at[strip], near.at[d], strip_send.at[d], strip_recv.at[d],
            device_id=to, device_id_type=MESH,
        )
        large = pltpu.make_async_remote_copy(
            source, target, send_sem.at[d], recv_sem.at[d], device_id=to, device_id_type=MESH
        )
        fill = None
        if dx:
            zeros = zero.at[pl.ds(0, 2)] if dy else zero
            fill = pltpu.make_async_copy(zeros, target, fill_sem.at[d])
        jobs.append((dy, dx, small, large, fill))

    for dy, dx, small, large, fill in jobs:

        @pl.when(there(dy, dx))
        def _():
            small.start()
            large.start()

    zero[...] = jnp.zeros_like(zero)
    for dy, dx, small, large, fill in jobs:

        if fill is None:
            continue

        @pl.when(jnp.logical_not(there(-dy, -dx)))
        def _():
            fill.start()
            fill.wait()

    for dy, dx, small, large, fill in jobs:

        @pl.when(there(dy, dx))
        def _():
            small.wait_send()
            large.wait_send()

        @pl.when(there(-dy, -dx))
        def _():
            small.wait_recv()
            large.wait_recv()


def exchange(vectors, masked):
    rows, cols, count = vectors.shape
    ny = lax.axis_size("gy")
    nx = lax.axis_size("gx")
    strips = jnp.stack([masked[:, 0, :], masked[:, -1, :], masked[:, :, 0], masked[:, :, -1]])
    strips = jnp.pad(strips, ((0, 0), (0, 7), (0, 128 - strips.shape[2])))
    any_space = pl.BlockSpec(memory_space=pl.ANY)
    real = jnp.float32
    sems = [pltpu.SemaphoreType.DMA((8,))] * 5
    up, down, left, right, near = pl.pallas_call(
        functools.partial(exchange_kernel, ny, nx),
        out_shape=(
            jax.ShapeDtypeStruct((2, cols, count), real),
            jax.ShapeDtypeStruct((2, cols, count), real),
            jax.ShapeDtypeStruct((rows + 4, 2, count), real),
            jax.ShapeDtypeStruct((rows + 4, 2, count), real),
            jax.ShapeDtypeStruct((8,) + strips.shape[1:], real),
        ),
        in_specs=[any_space] * 4,
        out_specs=(any_space,) * 5,
        scratch_shapes=[pltpu.VMEM((rows, 2, count), real)] + sems,
        compiler_params=pltpu.CompilerParams(collective_id=0, has_side_effects=True),
    )(vectors, vectors[:, :2], vectors[:, -2:], strips)
    gy = lax.axis_index("gy")
    gx = lax.axis_index("gx")
    found = {}
    for d, (dy, dx) in enumerate(DIRECTIONS):
        y = gy - dy
        x = gx - dx
        there = (y >= 0) & (y < ny) & (x >= 0) & (x < nx)
        strip = jnp.where(there, near[d, :9], 0)
        if dy == 0:
            found[dy, dx] = strip[:, :rows, None]
        elif dx == 0:
            found[dy, dx] = strip[:, None, :cols]
        else:
            at = cols - 1 if dx > 0 else 0
            found[dy, dx] = strip[:, None, at : at + 1]
    return (up, down, left, right), found


def masked_weights(coefficients):
    rows_dev = coefficients.shape[1]
    cols_dev = coefficients.shape[2]
    total_rows = rows_dev * lax.axis_size("gy")
    total_cols = cols_dev * lax.axis_size("gx")
    row_pos = lax.axis_index("gy") * rows_dev + jnp.arange(rows_dev, dtype=jnp.int32)[:, None]
    col_pos = lax.axis_index("gx") * cols_dev + jnp.arange(cols_dev, dtype=jnp.int32)[None, :]
    pieces = []
    for k in range(9):
        a = k // 3 - 1
        b = k % 3 - 1
        inside = (
            (row_pos + a >= 0)
            & (row_pos + a < total_rows)
            & (col_pos + b >= 0)
            & (col_pos + b < total_cols)
        )
        pieces.append(jnp.where(inside, coefficients[k], jnp.zeros_like(coefficients[k])))
    return jnp.stack(pieces)


def diagonals(ext, rows, cols, turned):
    terms = [None] * 25
    for k in range(9):
        a = k // 3 - 1
        b = k % 3 - 1
        if turned:
            at = (slice(1 - b, 1 - b + cols), slice(1 - a, 1 - a + rows))
        else:
            at = (slice(1 - a, 1 - a + rows), slice(1 - b, 1 - b + cols))
        first = ext[(k,) + at]
        for m in range(9):
            e = m // 3 - k // 3
            f = m % 3 - k % 3
            slot = (e + 2) * 5 + (f + 2)
            product = first * ext[(m,) + at]
            terms[slot] = product if terms[slot] is None else terms[slot] + product
    return terms


def band_kernel(rows, cols, ext_ref, turned_ref, normal_ref, high_ref, low_ref, halo_ref):
    for slot, term in enumerate(diagonals(ext_ref, rows, cols, False)):
        normal_ref[slot] = term
    columns = diagonals(turned_ref, rows, cols, True)
    deep = (GROUP + 4) * cols
    wide = (GROUP + 4) * 16
    shape = (cols, deep + wide)
    lane = lax.broadcasted_iota(jnp.int32, shape, 1)
    own = lax.broadcasted_iota(jnp.int32, shape, 0)
    beside = lane - deep
    is_main = lane < deep
    part = beside % 16
    near = part % 4
    source_row = jnp.where(is_main, lane // cols, beside // 16)
    source_col = jnp.where(is_main, lane % cols, jnp.where(near < 2, near - 2, near - 2 + cols))
    f = source_col - own
    usable = (f >= -2) & (f <= 2) & (is_main | (part < 12))
    takes_high = part < 8
    for rr in range(GROUP):
        e = source_row - 2 - rr
        code = jnp.where(usable & (e >= -2) & (e <= 2), (e + 2) * 5 + f + 2, -1)
        for r in range(rr, rows, GROUP):
            total = jnp.zeros(shape, jnp.float32)
            for slot in range(25):
                column = columns[slot][:, r : r + 1]
                total = jnp.where(code == slot, column, total)
            high = total.astype(jnp.bfloat16)
            rest = total - high.astype(jnp.float32)
            low = rest.astype(jnp.bfloat16)
            at = pl.ds(r * cols, cols)
            high_ref[at, :] = high[:, :deep]
            low_ref[at, :] = low[:, :deep]
            mixed = jnp.where(takes_high, high.astype(jnp.float32), rest)
            halo_ref[at, :] = mixed[:, deep:].astype(jnp.bfloat16)


def band_matrices(ext, rows, cols):
    deep = (GROUP + 4) * cols
    wide = (GROUP + 4) * 16
    cells = rows * cols
    turned = jnp.swapaxes(ext, 1, 2)
    return pl.pallas_call(
        functools.partial(band_kernel, rows, cols),
        out_shape=(
            jax.ShapeDtypeStruct((25, rows, cols), jnp.float32),
            jax.ShapeDtypeStruct((cells, deep), jnp.bfloat16),
            jax.ShapeDtypeStruct((cells, deep), jnp.bfloat16),
            jax.ShapeDtypeStruct((cells, wide), jnp.bfloat16),
        ),
        in_specs=[pl.BlockSpec(memory_space=pltpu.VMEM)] * 2,
        out_specs=(pl.BlockSpec(memory_space=pltpu.VMEM),) * 4,
        cost_estimate=pl.CostEstimate(flops=10_000_000, bytes_accessed=2_000_000, transcendentals=0),
    )(ext, turned)


def image_kernel(*refs):
    x_ref, up_ref, down_ref, left_ref, right_ref, high_ref, low_ref, mixed_ref = refs[:8]
    out_ref, xh, xl, side, xs = refs[8:]
    rows, cols, lanes = x_ref.shape

    @pl.when(pl.program_id(0) == 0)
    def _():
        side[...] = jnp.zeros_like(side)

    def place(row, block):
        high = block.astype(jnp.bfloat16)
        low = (block - high.astype(jnp.float32)).astype(jnp.bfloat16)
        xh[pl.ds(row, block.shape[0])] = high
        xl[pl.ds(row, block.shape[0])] = low

    gy = lax.axis_index("gy")
    has_up = gy > 0
    has_down = gy < lax.axis_size("gy") - 1
    place(0, jnp.where(has_up, up_ref[...], 0))
    place(rows + 2, jnp.where(has_down, down_ref[...], 0))
    for r in range(0, rows, 4):
        place(r + 2, x_ref[r : r + 4])
    for copy in range(3):
        side[:, pl.ds(4 * copy, 2)] = left_ref[...]
        side[:, pl.ds(4 * copy + 2, 2)] = right_ref[...]
    for r in range(0, rows + 4, 4):
        raw = side[r : r + 4]
        slot = lax.broadcasted_iota(jnp.int32, raw.shape, 1)
        high = raw.astype(jnp.bfloat16).astype(jnp.float32)
        value = jnp.where((slot >= 4) & (slot < 8), raw - high, high)
        xs[r : r + 4] = value.astype(jnp.bfloat16)
    dot = functools.partial(jnp.dot, preferred_element_type=jnp.float32)
    for g in range(rows // GROUP):
        at = pl.ds(g * GROUP * cols, GROUP * cols)
        span = pl.ds(g * GROUP, GROUP + 4)
        h = xh[span].reshape((GROUP + 4) * cols, lanes)
        l = xl[span].reshape((GROUP + 4) * cols, lanes)
        s = xs[span].reshape((GROUP + 4) * 16, lanes)
        total = dot(high_ref[at, :], h) + dot(low_ref[at, :], h)
        total = total + dot(high_ref[at, :], l) + dot(mixed_ref[at, :], s)
        out_ref[pl.ds(g * GROUP, GROUP)] = total.reshape(GROUP, cols, lanes)


def image_of(vectors, halos, bands):
    rows, cols, count = vectors.shape
    blocks = [vectors, *halos]
    cells = rows * cols * count
    return pl.pallas_call(
        image_kernel,
        grid=(count // LANES,),
        out_shape=jax.ShapeDtypeStruct(vectors.shape, vectors.dtype),
        in_specs=[pl.BlockSpec(h.shape[:2] + (LANES,), lambda j: (0, 0, j)) for h in blocks]
        + [pl.BlockSpec(b.shape, lambda j: (0, 0)) for b in bands],
        out_specs=pl.BlockSpec((rows, cols, LANES), lambda j: (0, 0, j)),
        scratch_shapes=[
            pltpu.VMEM((rows + 4, cols, LANES), jnp.bfloat16),
            pltpu.VMEM((rows + 4, cols, LANES), jnp.bfloat16),
            pltpu.VMEM((rows + 4, 16, LANES), jnp.float32),
            pltpu.VMEM((rows + 4, 16, LANES), jnp.bfloat16),
        ],
        cost_estimate=pl.CostEstimate(flops=cells * 2048, bytes_accessed=cells * 8, transcendentals=0),
        compiler_params=pltpu.CompilerParams(dimension_semantics=("arbitrary",)),
    )(*blocks, *bands)


def per_device(coefficients, vectors):
    rows, cols, _ = vectors.shape
    masked = masked_weights(coefficients)
    halos, near = exchange(vectors, masked)
    ext = jnp.concatenate(
        [
            jnp.concatenate([near[dy, 1], near[dy, 0] if dy else masked, near[dy, -1]], axis=2)
            for dy in (1, 0, -1)
        ],
        axis=1,
    )
    normal, *bands = band_matrices(ext, rows, cols)
    image = image_of(vectors, halos, bands)
    return (normal, image)


def solution(mesh):
    in_specs = (P(None, "gy", "gx"), P("gy", "gx", None))
    out_specs = (P(None, "gy", "gx"), P("gy", "gx", None))
    return jax.shard_map(
        per_device, mesh=mesh, in_specs=in_specs, out_specs=out_specs, check_vma=False
    )
```

profile of v0, /device:TPU:1, one launch (start us, length us, event | category | flops | bytes accessed | tf_op | source)
XLA Modules:
  0.0 50.0 jit_solution(4403568427896412737)
XLA Ops:
  0.7 0.9 %fusion.10 = (f32[1,32,32]{2,1,0:T(8,128)S(1)}, f32[1,32,32]{2,1,0:T(8,128)S(1)}, f32[1,32,32]{2,1,0:T(8,128)S(1)}, f32[1,32,32]{2,1,0:T(8,128)S(1)}, f32[1,32,3...) fusion(f32[9,32,32]{2,1,0:T(8,128)} %param.2), kind=kLoop, calls=%fused_computation.44 | loop fusion | bytes 73728 | tf_op jit(solution)/shard_map/slice | solution.py:154
  2.3 0.1 constant_dynamic-update-slice_fusion.7
  2.5 0.1 constant_dynamic-update-slice_fusion.6
  2.5 0.1 constant_dynamic-update-slice_fusion.5
  2.6 0.1 constant_dynamic-update-slice_fusion.4
  2.7 0.1 constant_dynamic-update-slice_fusion.3
  2.9 0.1 constant_dynamic-update-slice_fusion.1
  2.9 0.1 constant_dynamic-update-slice_fusion
  3.0 0.1 fusion.9
  3.1 0.1 copy.94
  3.3 0.1 copy.95
  3.4 0.6 %pad.4.clone.strips_ref = f32[4,16,128]{2,1,0:T(8,128)} pad(f32[4,9,32]{2,1,0:T(8,128)S(1)} %copy.96, f32[]{:T(128)} %constant.10.clone.1), padding=0_0x0_7x0_96 | pad | bytes 37380 | tf_op jit(solution)/shard_map/jit(_pad)/pad | solution.py:101
  4.1 3.7 %fusion.8 = (f32[32,2,2048]{2,1,0:T(2,128)}, f32[32,2,2048]{2,1,0:T(2,128)}) fusion(f32[32,32,2048]{2,1,0:T(8,128)} %refs_0_.1), kind=kLoop, calls=%fused_computation.42 | loop fusion | bytes 2097152 | tf_op jit(solution)/shard_map/slice | solution.py:118
  7.7 19.9 %shard_map.41 = (f32[2,32,2048]{2,1,0:T(8,128)}, f32[2,32,2048]{2,1,0:T(8,128)}, f32[36,2,2048]{2,1,0:T(2,128)}, f32[36,2,2048]{2,1,0:T(2,128)}, f32[8,16,128]{2,1,0:T(8,128)}) custom-call(f32[32,32,2048]{2,1,0:T(8,128)} %refs_0_.1, f32[32,2,2048]{2,1,0:T(2,128)} %get-tuple-element.21.first_ref, f32[32,2,2048]{2,1,0:T(2,128)} %get-tuple-element.20.last_ref, ...), custom_call_target="tpu_custom_call" | custom-call | tf_op jit(solution)/shard_map/pallas_call | solution.py:105
  27.6 0.8 %select_bitcast_fusion.7 = (f32[9,128]{1,0:T(8,128)S(1)}, f32[9,128]{1,0:T(8,128)S(1)}, f32[9,128]{1,0:T(8,128)S(1)}, f32[9,128]{1,0:T(8,128)S(1)}, f32[9,128]{1...) fusion(f32[8,16,128]{2,1,0:T(8,128)} %get-tuple-element.11, pred[]{:T(512)S(6)} %and.375, ...), kind=kLoop, calls=%fused_computation.26 | loop fusion | flops 9216 | bytes 73736 | tf_op jit(solution)/shard_map/jit(_where)/select_n | solution.py:126
  28.6 0.1 slice_reduce_fusion
  28.7 0.2 slice_reduce_fusion.1
  29.2 0.1 copy.81
  29.3 0.2 copy.83
  29.5 0.9 %fusion.11.turned_ref = f32[9,34,34]{2,1,0:T(8,128)} fusion(f32[9,1,1]{1,2,0:T(1,128)S(1)} %broadcast_in_dim.47, f32[9,1,32]{1,2,0:T(8,128)S(1)} %copy.81, f32[9,1,1]{1,2,0:T(1,128)S(1)} %broadcast_in_dim.46, f32[9,32,1]{1,2,0:T(1,128)S(1)} %broadcast_in_dim.42, f32[9,32,32]{1,2,0:T(8,128)S(1)} %constant_dynamic-update-slice_fusion, ...), kind=kLoop, calls=%fused_computation.45 | loop fusion | flops 62424 | bytes 83232 | tf_op jit(solution)/shard_map/transpose | solution.py:217
  30.3 0.2 maximum_maximum_fusion
  30.5 0.8 %copy.84.ext_ref = f32[9,34,34]{2,1,0:T(8,128)} copy(f32[9,34,34]{1,2,0:T(8,128)S(1)} %maximum_maximum_fusion) | data formatting | bytes 83232 | tf_op jit(solution)/shard_map/concatenate | solution.py:301
  31.4 6.8 %shard_map.42 = (f32[25,32,32]{2,1,0:T(8,128)}, bf16[1024,256]{1,0:T(8,128)(2,1)}, bf16[1024,256]{1,0:T(8,128)(2,1)}, bf16[1024,128]{1,0:T(8,128)(2,1)}) custom-call(f32[9,34,34]{2,1,0:T(8,128)} %copy.84.ext_ref, f32[9,34,34]{2,1,0:T(8,128)} %fusion.11.turned_ref), custom_call_target="tpu_custom_call" | custom-call | flops 10000000 | bytes 2000000 | tf_op jit(solution)/shard_map/pallas_call | solution.py:218
  38.1 11.9 %shard_map.43 = f32[32,32,2048]{2,1,0:T(8,128)} custom-call(f32[32,32,2048]{2,1,0:T(8,128)} %refs_0_.1, f32[2,32,2048]{2,1,0:T(8,128)} %get-tuple-element.13.refs_1_, f32[2,32,2048]{2,1,0:T(8,128)} %get-tuple-element.14.refs_2_, f32[36,2,2048]{2,1,0:T(2,128)} %get-tuple-element.15.refs_3_, f32[36,2,2048]{2,1,0:T(2,128)} %get-tuple-element.16.refs_4_, ...), custom_call_target="tpu_custom_call" | custom-call | flops 4294967296 | bytes 16777216 | tf_op jit(solution)/shard_map/pallas_call | solution.py:279
  (29 shorter events, 1.2 us)
where the time goes:
time: 50.5 us; the launch traced here: 50 us
  Pallas kernels  38.5 us (76%)
  local copies, waits for them, and re-layouts  7.82 us (15%)
  other arithmetic  2.82 us (6%)
  between operations  0.81 us (2%)
    pallas_call x1, Pallas kernels, exchange(): pl.pallas_call(functools.partial(exchange_kernel, ny, nx), out_shape=(jax...  19.9 us
    pallas_call x1, Pallas kernels, image_of(): pl.pallas_call(image_kernel, grid=(count // LANES,), out_shape=jax.ShapeD...  11.9 us
    pallas_call x1, Pallas kernels, band_matrices(): pl.pallas_call(functools.partial(band_kernel, rows, cols), out_shape=(jax...  6.75 us
    slice x1, local copies, waits for them, and re-layouts, exchange(): vectors[:, -2:]  3.67 us

commit v1 on v0

--- a/solution.py
+++ b/solution.py
@@ -14,9 +14,9 @@
 DIRECTIONS = ((1, 0), (-1, 0), (0, 1), (0, -1), (1, 1), (1, -1), (-1, 1), (-1, -1))
 
 
-def exchange_kernel(ny, nx, x_ref, first_ref, last_ref, strips_ref, up, down, left, right, near, zero, *sems):
+def exchange_kernel(ny, nx, x_ref, strips_ref, up, down, left, right, near, zero, *sems):
     send_sem, recv_sem, strip_send, strip_recv, fill_sem = sems
-    rows = x_ref.shape[0]
+    rows, cols, _ = x_ref.shape
     gy = lax.axis_index("gy")
     gx = lax.axis_index("gx")
 
@@ -45,8 +45,8 @@
             source = x_ref.at[mine[dy]]
             target = up if dy > 0 else down
         else:
-            column = last_ref if dx > 0 else first_ref
-            source = column.at[mine[dy]] if dy else column
+            lines = mine[dy] if dy else pl.ds(0, rows)
+            source = x_ref.at[lines, pl.ds(cols - 2 if dx > 0 else 0, 2)]
             target = (left if dx > 0 else right).at[land[dy]]
         strip = (dy + 1) // 2 if dy else 2 + (dx + 1) // 2
         small = pltpu.make_async_remote_copy(
@@ -111,11 +111,11 @@
             jax.ShapeDtypeStruct((rows + 4, 2, count), real),
             jax.ShapeDtypeStruct((8,) + strips.shape[1:], real),
         ),
-        in_specs=[any_space] * 4,
+        in_specs=[any_space] * 2,
         out_specs=(any_space,) * 5,
         scratch_shapes=[pltpu.VMEM((rows, 2, count), real)] + sems,
         compiler_params=pltpu.CompilerParams(collective_id=0, has_side_effects=True),
-    )(vectors, vectors[:, :2], vectors[:, -2:], strips)
+    )(vectors, strips)
     gy = lax.axis_index("gy")
     gx = lax.axis_index("gx")
     found = {}
@@ -195,11 +195,18 @@
     for rr in range(GROUP):
         e = source_row - 2 - rr
         code = jnp.where(usable & (e >= -2) & (e <= 2), (e + 2) * 5 + f + 2, -1)
+        codes = [code[:, n : n + 128] for n in range(0, deep + wide, 128)]
         for r in range(rr, rows, GROUP):
-            total = jnp.zeros(shape, jnp.float32)
+            parts = [jnp.zeros((cols, 128), jnp.float32)] * len(codes)
             for slot in range(25):
                 column = columns[slot][:, r : r + 1]
-                total = jnp.where(code == slot, column, total)
+                line = slot // 5 + rr
+                touched = {line * cols // 128, (line * cols + cols - 1) // 128}
+                if slot % 5 != 2:
+                    touched.add((deep + line * 16) // 128)
+                for n in sorted(touched):
+                    parts[n] = jnp.where(codes[n] == slot, column, parts[n])
+            total = jnp.concatenate(parts, axis=1)
             high = total.astype(jnp.bfloat16)
             rest = total - high.astype(jnp.float32)
             low = rest.astype(jnp.bfloat16)

time: 50.5 us -> 46.2 us (0.915)
  local copies, waits for them, and re-layouts: 7.82 us -> 4.15 us
    slice x1 -> x0, local copies, waits for them, and re-layouts: 3.67 us -> none  [exchange(): vectors[:, -2:]]
    pallas_call x1, Pallas kernels: 6.75 us -> 6.22 us  [band_matrices(): pl.pallas_call(functools.partial(band_kernel, rows, cols), out_shape=(jax...]
where the time goes in v1:
time: 46.2 us; the launch traced here: 45.8 us
  Pallas kernels  38 us (82%)
  local copies, waits for them, and re-layouts  4.15 us (9%)
  other arithmetic  2.82 us (6%)
  between operations  0.81 us (2%)
    pallas_call x1, Pallas kernels, exchange(): pl.pallas_call(functools.partial(exchange_kernel, ny, nx), out_shape=(jax...  19.9 us
    pallas_call x1, Pallas kernels, image_of(): pl.pallas_call(image_kernel, grid=(count // LANES,), out_shape=jax.ShapeD...  11.9 us
    pallas_call x1, Pallas kernels, band_matrices(): pl.pallas_call(functools.partial(band_kernel, rows, cols), out_shape=(jax...  6.22 us

profile of v1, /device:TPU:1, one launch (start us, length us, event | category | flops | bytes accessed | tf_op | source)
XLA Modules:
  0.0 45.8 jit_solution(12170151510670108351)
XLA Ops:
  0.7 0.9 %fusion.9 = (f32[1,32,32]{2,1,0:T(8,128)S(1)}, f32[1,32,32]{2,1,0:T(8,128)S(1)}, f32[1,32,32]{2,1,0:T(8,128)S(1)}, f32[1,32,32]{2,1,0:T(8,128)S(1)}, f32[1,32,32...) fusion(f32[9,32,32]{2,1,0:T(8,128)} %param.2), kind=kLoop, calls=%fused_computation.43 | loop fusion | bytes 73728 | tf_op jit(solution)/shard_map/slice | solution.py:154
  2.3 0.1 constant_dynamic-update-slice_fusion.7
  2.5 0.1 constant_dynamic-update-slice_fusion.6
  2.5 0.1 constant_dynamic-update-slice_fusion.5
  2.6 0.1 constant_dynamic-update-slice_fusion.4
  2.7 0.1 constant_dynamic-update-slice_fusion.3
  2.8 0.1 constant_dynamic-update-slice_fusion.2
  2.9 0.1 constant_dynamic-update-slice_fusion.1
  2.9 0.1 constant_dynamic-update-slice_fusion
  3.0 0.1 fusion.8
  3.1 0.1 copy.94
  3.3 0.1 copy.95
  3.4 0.6 %pad.4.clone.strips_ref = f32[4,16,128]{2,1,0:T(8,128)} pad(f32[4,9,32]{2,1,0:T(8,128)S(1)} %copy.96, f32[]{:T(128)} %constant.10.clone.1), padding=0_0x0_7x0_96 | pad | bytes 37380 | tf_op jit(solution)/shard_map/jit(_pad)/pad | solution.py:101
  4.1 19.9 %shard_map.41 = (f32[2,32,2048]{2,1,0:T(8,128)}, f32[2,32,2048]{2,1,0:T(8,128)}, f32[36,2,2048]{2,1,0:T(2,128)}, f32[36,2,2048]{2,1,0:T(2,128)}, f32[8,16,128]{2,1,0:T(8,128)}) custom-call(f32[32,32,2048]{2,1,0:T(8,128)} %refs_0_.1, f32[4,16,128]{2,1,0:T(8,128)} %pad.4.clone.strips_ref), custom_call_target="tpu_custom_call" | custom-call | tf_op jit(solution)/shard_map/pallas_call | solution.py:105
  24.0 0.8 %select_bitcast_fusion.7 = (f32[9,128]{1,0:T(8,128)S(1)}, f32[9,128]{1,0:T(8,128)S(1)}, f32[9,128]{1,0:T(8,128)S(1)}, f32[9,128]{1,0:T(8,128)S(1)}, f32[9,128]{1...) fusion(f32[8,16,128]{2,1,0:T(8,128)} %get-tuple-element.11, pred[]{:T(512)S(6)} %and.375, ...), kind=kLoop, calls=%fused_computation.26 | loop fusion | flops 9216 | bytes 73736 | tf_op jit(solution)/shard_map/jit(_where)/select_n | solution.py:126
  24.9 0.1 slice_reduce_fusion
  25.0 0.2 slice_reduce_fusion.1
  25.5 0.1 copy.81
  25.6 0.2 copy.83
  25.8 0.9 %fusion.10.turned_ref = f32[9,34,34]{2,1,0:T(8,128)} fusion(f32[9,1,1]{1,2,0:T(1,128)S(1)} %broadcast_in_dim.47, f32[9,1,32]{1,2,0:T(8,128)S(1)} %copy.81, f32[9,1,1]{1,2,0:T(1,128)S(1)} %broadcast_in_dim.46, f32[9,32,1]{1,2,0:T(1,128)S(1)} %broadcast_in_dim.42, f32[9,32,32]{1,2,0:T(8,128)S(1)} %constant_dynamic-update-slice_fusion, ...), kind=kLoop, calls=%fused_computation.44 | loop fusion | flops 62424 | bytes 83232 | tf_op jit(solution)/shard_map/transpose | solution.py:224
  26.7 0.2 maximum_maximum_fusion
  26.9 0.8 %copy.84.ext_ref = f32[9,34,34]{2,1,0:T(8,128)} copy(f32[9,34,34]{1,2,0:T(8,128)S(1)} %maximum_maximum_fusion) | data formatting | bytes 83232 | tf_op jit(solution)/shard_map/concatenate | solution.py:308
  27.7 6.2 %shard_map.42 = (f32[25,32,32]{2,1,0:T(8,128)}, bf16[1024,256]{1,0:T(8,128)(2,1)}, bf16[1024,256]{1,0:T(8,128)(2,1)}, bf16[1024,128]{1,0:T(8,128)(2,1)}) custom-call(f32[9,34,34]{2,1,0:T(8,128)} %copy.84.ext_ref, f32[9,34,34]{2,1,0:T(8,128)} %fusion.10.turned_ref), custom_call_target="tpu_custom_call" | custom-call | flops 10000000 | bytes 2000000 | tf_op jit(solution)/shard_map/pallas_call | solution.py:225
  33.9 11.9 %shard_map.43 = f32[32,32,2048]{2,1,0:T(8,128)} custom-call(f32[32,32,2048]{2,1,0:T(8,128)} %refs_0_.1, f32[2,32,2048]{2,1,0:T(8,128)} %get-tuple-element.13.refs_1_, f32[2,32,2048]{2,1,0:T(8,128)} %get-tuple-element.14.refs_2_, f32[36,2,2048]{2,1,0:T(2,128)} %get-tuple-element.15.refs_3_, f32[36,2,2048]{2,1,0:T(2,128)} %get-tuple-element.16.refs_4_, ...), custom_call_target="tpu_custom_call" | custom-call | flops 4294967296 | bytes 16777216 | tf_op jit(solution)/shard_map/pallas_call | solution.py:286
  (28 shorter events, 1.2 us)
